TPU v7x, 32 devices: a whole 2x2x4 slice. The times are simulated.
32 devices in a mesh: rep: 1, dp: 32 (over x, y, z, core).
Axes of the slice: x: 2, y: 2, z: 4, core: 2. Of those that a mesh axis runs over, the one named last changes fastest.
Arguments:
- a: bfloat16 [32, 2, 4096, 1280], P(('rep', 'dp'))
- g: bfloat16 [32, 2, 4096, 5120], P(('rep', 'dp'))
Outputs:
- output: bfloat16 [2, 1280, 5120], P('rep')
All inputs are finite; a program needn't handle non-finite values.
Results may differ from a plain program's by a relative error of at most 0.012.
Values are sent between devices in bfloat16 or wider.
A program may use at most 2 GiB of HBM per device.

v0:
```python
import jax
import jax.numpy as jnp


def solution(mesh):
    groups = mesh.shape["rep"]

    def step(a, g):
        a, g = (t.reshape(groups, -1, *t.shape[1:]) for t in (a, g))
        sums = jnp.einsum("rsntd,rsntf->rndf", a, g, preferred_element_type=jnp.float32)
        return sums.astype(jnp.bfloat16).reshape(-1, *sums.shape[2:])

    return step
```

profile of v0, /device:TPU:0, one launch (start us, length us, event | category | flops | bytes accessed | tf_op | source)
XLA Modules:
  0.0 946.4 jit_solution(10433833540177866278)
XLA Ops:
  0.0 120.5 %fusion = f32[2,1280,5120]{2,1,0:T(8,128)} fusion(bf16[1,2,4096,5120]{3,2,1,0:T(8,128)(2,1)} %param.1, bf16[1,2,4096,1280]{3,2,1,0:T(8,128)(2,1)} %param), kind=kOutput, calls=%fused_computation | convolution fusion | flops 107374182400 | bytes 157286400 | tf_op jit(solution)/rsntd,rsntf->rndf/dot_general | solution.py:10
  120.5 826.0 %all-reduce.2 = bf16[2,1280,5120]{2,1,0:T(8,128)(2,1)} all-reduce(f32[2,1280,5120]{2,1,0:T(8,128)} %fusion), channel_id=1, replica_groups=mesh['axis_0'=32] {'axis_0'}, use_global_device_ids=true, to_apply=%add.clone | all-reduce | flops 13107200 | bytes 78643200 | tf_op jit(solution)/rsntd,rsntf->rndf/dot_general | solution.py:10
where the time goes:
time: 947 us; the launch traced here: 946 us
  blocking collectives  826 us (87%)
  matrix products  120 us (13%)
    dot_general x1, blocking collectives, step(): jnp.einsum('rsntd,rsntf->rndf', a, g, preferred_element_type=jnp.float32)  826 us
    dot_general x1, matrix products, step(): jnp.einsum('rsntd,rsntf->rndf', a, g, preferred_element_type=jnp.float32)  120 us

commit v1 on v0

v1 whole, which is shorter than its diff:
```python
import functools

import jax
import jax.numpy as jnp
from jax import lax
from jax.experimental import pallas as pl
from jax.experimental.pallas import tpu as pltpu
from jax.sharding import PartitionSpec as P

MESH = pl.DeviceIdType.MESH
F32, BF16 = jnp.float32, jnp.bfloat16
CREDITS = 3
KEPT = 10
S1, S2, S3, S4, S5, S6, S7 = 4, 8, 12, 16, 20, 23, 27
HOP = 4


def kernel(width, stage, a_ref, g_ref, o_ref, aT, ast, gbuf, send0, recv0, mL, mK, sendA, recvA, sendR, sendL, recvR,
           recvL, sendB, recvB, fin, a_sem, g_sem, s0, r0, sA, rA, sR, rR, sL, rL, sB, rB, lc, gBs, gB, gZs, gZ, gAs,
           gA, gCs, gC, credit):
    me = lax.axis_index("dp")
    core, z = lax.rem(me, 2), lax.rem(me // 2, 4)
    y, x = lax.rem(me // 8, 2), me // 16
    partner = me + 1 - 2 * core
    over_x, over_y = me + 16 * (1 - 2 * x), me + 8 * (1 - 2 * y)
    over_A = over_x * (1 - core) + over_y * core
    over_B = over_y * (1 - core) + over_x * core
    al, be = x * (1 - core) + y * core, y * (1 - core) + x * core
    up, down = me + 2, me - 2
    mats, depth, rows = a_ref.shape[1:]
    per = g_ref.shape[3] // width
    chunks = mats * per
    half, quarter, piece, leaf = rows // 2, rows // 4, rows // 8, rows // 16
    mine, keep = core * half, core * half + al * quarter
    end = 1 - z // 3
    is_end = (z == 0) | (z == 3)

    def at(c, first, count):
        cols = pl.ds(pl.multiple_of(lax.rem(c, per) * width, width), width)
        return o_ref.at[c // per, pl.ds(pl.multiple_of(first, leaf), count), cols]

    def rdma(src, dst, ssem, rsem, to):
        return pltpu.make_async_remote_copy(src_ref=src, dst_ref=dst, send_sem=ssem, recv_sem=rsem, device_id={"dp": to},
                                            device_id_type=MESH)

    def by_rows(count, block, f):
        @pl.loop(0, count // block)
        def _(i):
            f(pl.multiple_of(i * block, block))

    blk = leaf

    def load_a(n, k):
        return pltpu.make_async_copy(a_ref.at[0, n, pl.ds(pl.multiple_of(k * stage, stage), stage), :],
                                     ast.at[lax.rem(k, 2)], a_sem.at[lax.rem(k, 2)])

    def load_g(t):
        cols = pl.ds(pl.multiple_of(lax.rem(t, per) * width, width), width)
        return pltpu.make_async_copy(g_ref.at[0, t // per, :, cols], gbuf.at[lax.rem(t, 2)], g_sem.at[lax.rem(t, 2)])

    def transpose_a(n):
        @pl.loop(0, depth // stage)
        def _(k):
            load_a(n, k).wait()
            aT[:, pl.ds(pl.multiple_of(k * stage, stage), stage)] = ast[lax.rem(k, 2)].T

            @pl.when(k + 2 < depth // stage)
            def _():
                load_a(n, k + 2).start()

    def product(t, first):
        return jnp.dot(aT[pl.ds(pl.multiple_of(first, quarter), quarter), :], gbuf[lax.rem(t, 2)],
                       preferred_element_type=F32)

    def copy0(c):
        return rdma(send0.at[lax.rem(c, 2)], recv0.at[lax.rem(c, CREDITS)], s0.at[lax.rem(c, 2)],
                    r0.at[lax.rem(c, CREDITS)], partner)

    def copyA(c):
        return rdma(sendA.at[lax.rem(c, 2)], recvA.at[c], sA.at[lax.rem(c, 2)], rA.at[c], over_A)

    def copyR(c):
        return rdma(sendR.at[lax.rem(c, 2)], recvR.at[c], sR.at[lax.rem(c, 2)], rR.at[c], up)

    def copyL(c):
        return rdma(sendL.at[lax.rem(c, 2)], recvL.at[c], sL.at[lax.rem(c, 2)], rL.at[c], down)

    def copyB(c):
        return rdma(sendB.at[lax.rem(c, 2)], recvB.at[c], sB.at[lax.rem(c, 2)], rB.at[c], over_B)

    def reuse(c, copy):
        @pl.when(c >= 2)
        def _():
            copy(c - 2).wait_send()

    def own_leaf(c):
        return at(c, keep + end * piece + be * leaf, leaf)

    def copy_own(c):
        return pltpu.make_async_copy(fin.at[lax.rem(c, 2)], own_leaf(c), lc.at[lax.rem(c, 2)])

    def give_leaf(c):
        return rdma(fin.at[lax.rem(c, 2)], own_leaf(c), gBs.at[lax.rem(c, 2)], gB.at[c], over_B)

    def take_leaf(c):
        there = at(c, keep + end * piece + (1 - be) * leaf, leaf)
        return rdma(there, there, gBs.at[lax.rem(c, 2)], gB.at[c], over_B)

    def stage1(c):
        copy0(c).wait_recv()
        reuse(c, copyA)

        def leaving(i):
            old = recv0[lax.rem(c, CREDITS), pl.ds(pl.multiple_of((1 - al) * quarter + i, blk), blk), :].astype(F32)
            sendA[lax.rem(c, 2), pl.ds(i, blk), :] = (mL[pl.ds(i, blk), :] + old).astype(BF16)

        by_rows(quarter, blk, leaving)
        copyA(c).start()

        def kept(i):
            old = recv0[lax.rem(c, CREDITS), pl.ds(pl.multiple_of(al * quarter + i, blk), blk), :].astype(F32)
            mK[lax.rem(c, KEPT), pl.ds(i, blk), :] += old

        by_rows(quarter, blk, kept)

        @pl.when(c + CREDITS < chunks)
        def _():
            pl.semaphore_signal(credit, inc=1, device_id={"dp": partner}, device_id_type=MESH)

    def pass_on(c, first, arrived, send, copy):
        reuse(c, copy)

        def add(i):
            total = mK[lax.rem(c, KEPT), pl.ds(first + i, blk), :]
            if arrived is not None:
                total = total + arrived[c, pl.ds(i, blk), :].astype(F32)
            send[lax.rem(c, 2), pl.ds(i, blk), :] = total.astype(BF16)

        by_rows(piece, blk, add)
        copy(c).start()

    def stage2(c):
        copyA(c).wait_recv()

        def add(i):
            mK[lax.rem(c, KEPT), pl.ds(i, blk), :] += recvA[c, pl.ds(i, blk), :].astype(F32)

        by_rows(quarter, blk, add)

        @pl.when(z == 0)
        def _():
            pass_on(c, 0, None, sendR, copyR)

        @pl.when(z == 3)
        def _():
            pass_on(c, piece, None, sendL, copyL)

    def hop_up(c):
        copyR(c).wait_recv()
        pass_on(c, 0, recvR, sendR, copyR)

    def hop_down(c):
        copyL(c).wait_recv()
        pass_on(c, piece, recvL, sendL, copyL)

    def stage3(c):
        pl.when(z == 1)(lambda: hop_up(c))
        pl.when(z == 2)(lambda: hop_down(c))

    def stage4(c):
        pl.when(z == 2)(lambda: hop_up(c))
        pl.when(z == 1)(lambda: hop_down(c))

    def finish_z(c, first, arrived, copy):
        copy(c).wait_recv()
        reuse(c, copyB)

        def out(i):
            total = mK[lax.rem(c, KEPT), pl.ds(pl.multiple_of(first + (1 - be) * leaf, leaf), leaf), :]
            total = total + arrived[c, pl.ds(pl.multiple_of((1 - be) * leaf, leaf), leaf), :].astype(F32)
            sendB[lax.rem(c, 2)] = total.astype(BF16)

        out(0)
        copyB(c).start()
        own = pl.ds(pl.multiple_of(first + be * leaf, leaf), leaf)
        mK[lax.rem(c, KEPT), own, :] += arrived[c, pl.ds(pl.multiple_of(be * leaf, leaf), leaf), :].astype(F32)

    def stage5(c):
        pl.when(z == 3)(lambda: finish_z(c, 0, recvR, copyR))
        pl.when(z == 0)(lambda: finish_z(c, piece, recvL, copyL))

    def stage6(c):
        @pl.when(is_end)
        def _():
            copyB(c).wait_recv()
            reuse(c, give_leaf)
            own = pl.ds(pl.multiple_of(end * piece + be * leaf, leaf), leaf)
            fin[lax.rem(c, 2)] = (mK[lax.rem(c, KEPT), own, :] + recvB[c].astype(F32)).astype(BF16)
            give_leaf(c).start()
            copy_own(c).start()

    def to_z(c, d):
        here = at(c, keep + d * piece, piece)
        return rdma(here, here, gZs.at[d], gZ.at[c, d], up if d else down)

    def to_A(c, d):
        here = at(c, keep + d * piece, piece)
        return rdma(here, here, gAs, gA.at[c, d], over_A)

    def from_A(c, d):
        there = at(c, mine + (1 - al) * quarter + d * piece, piece)
        return rdma(there, there, gAs, gA.at[c, d], over_A)

    def to_core(c, first):
        here = at(c, first, piece)
        return rdma(here, here, gCs, gC, partner)

    def far(d):
        return z if d else 3 - z

    def have(c, d, hop):
        if hop < 3:
            to_z(c, d).start()
        to_A(c, d).start()
        to_core(c, keep + d * piece).start()

    def stage7(hop, c):
        for d in (0, 1):
            @pl.when(far(d) == hop)
            def _(d=d):
                if hop == 0:
                    take_leaf(c).wait_recv()
                    copy_own(c).wait()
                else:
                    to_z(c, d).wait_recv()
                have(c, d, hop)

    def stage8(hop, c):
        for d in (0, 1):
            @pl.when(far(d) == hop)
            def _(d=d):
                from_A(c, d).wait_recv()
                to_core(c, mine + (1 - al) * quarter + d * piece).start()

    stages = [(S1, stage1), (S2, stage2), (S3, stage3), (S4, stage4), (S5, stage5), (S6, stage6)]
    stages += [(S7 + HOP * hop, functools.partial(stage7, hop)) for hop in range(4)]
    stages += [(S7 + HOP * hop + HOP, functools.partial(stage8, hop)) for hop in range(4)]
    last = max(lag for lag, _ in stages) // 4

    def serve(t, q):
        for lag, f in sorted(stages, key=lambda s: -s[0]):
            if lag % 4 == q:
                c = t - lag // 4

                @pl.when((c >= 0) & (c < chunks))
                def _(f=f, c=c):
                    f(c)

    load_a(0, 0).start()
    load_a(0, 1).start()
    load_g(0).start()

    @pl.loop(0, chunks + last)
    def _(t):
        @pl.when(t + 1 < chunks)
        def _():
            load_g(t + 1).start()

        serve(t, 0)

        @pl.when(t < chunks)
        def _():
            @pl.when(lax.rem(t, per) == 0)
            def _():
                transpose_a(t // per)

            @pl.when((lax.rem(t, per) == per - 1) & (t + 1 < chunks))
            def _():
                load_a(t // per + 1, 0).start()
                load_a(t // per + 1, 1).start()

            load_g(t).wait()
            reuse(t, copy0)
            send0[lax.rem(t, 2), pl.ds(0, quarter), :] = product(t, (1 - core) * half).astype(BF16)

        serve(t, 1)

        @pl.when(t < chunks)
        def _():
            send0[lax.rem(t, 2), pl.ds(quarter, quarter), :] = product(t, (1 - core) * half + quarter).astype(BF16)

            @pl.when(t >= CREDITS)
            def _():
                pl.semaphore_wait(credit, 1)

            copy0(t).start()

        serve(t, 2)

        @pl.when(t < chunks)
        def _():
            mL[...] = product(t, mine + (1 - al) * quarter)

        serve(t, 3)

        @pl.when(t < chunks)
        def _():
            mK[lax.rem(t, KEPT)] = product(t, keep)

    def rest(first, count):
        return o_ref.at[:, pl.ds(pl.multiple_of(first, leaf), count), :]

    for c in range(chunks - 2, chunks):
        copy0(c).wait_send()
        copyA(c).wait_send()
        pl.when(z < 3)(lambda: copyR(c).wait_send())
        pl.when(z > 0)(lambda: copyL(c).wait_send())

        @pl.when(is_end)
        def _(c=c):
            copyB(c).wait_send()
            give_leaf(c).wait_send()

    for d in (0, 1):
        @pl.when(far(d) < 3)
        def _(d=d):
            some = rest(keep + d * piece, piece)
            rdma(some, some, gZs.at[d], gC, partner).wait_send()

    some = rest(keep, quarter)
    rdma(some, some, gAs, gC, over_A).wait_send()
    some = rest(mine, half)
    rdma(some, some, gCs, gC, partner).wait_send()
    some = rest((1 - core) * half, half)
    rdma(some, some, gCs, gC, partner).wait_recv()


def solution(mesh, width=512, stage=512):
    def step(a, g):
        mats, depth, rows = a.shape[1:]
        columns = g.shape[3]
        chunks = mats * (columns // width)
        half, quarter, piece, leaf = rows // 2, rows // 4, rows // 8, rows // 16
        dma = pltpu.SemaphoreType.DMA
        return pl.pallas_call(
            functools.partial(kernel, width, stage),
            out_shape=jax.ShapeDtypeStruct((mats, rows, columns), BF16),
            in_specs=[pl.BlockSpec(memory_space=pl.ANY)] * 2,
            out_specs=pl.BlockSpec(memory_space=pl.ANY),
            scratch_shapes=[
                pltpu.VMEM((rows, depth), BF16),
                pltpu.VMEM((2, stage, rows), BF16),
                pltpu.VMEM((2, depth, width), BF16),
                pltpu.VMEM((2, half, width), BF16),
                pltpu.VMEM((CREDITS, half, width), BF16),
                pltpu.VMEM((quarter, width), F32),
                pltpu.VMEM((KEPT, quarter, width), F32),
                pltpu.VMEM((2, quarter, width), BF16),
                pltpu.VMEM((chunks, quarter, width), BF16),
                pltpu.VMEM((2, piece, width), BF16),
                pltpu.VMEM((2, piece, width), BF16),
                pltpu.VMEM((chunks, piece, width), BF16),
                pltpu.VMEM((chunks, piece, width), BF16),
                pltpu.VMEM((2, leaf, width), BF16),
                pltpu.VMEM((chunks, leaf, width), BF16),
                pltpu.VMEM((2, leaf, width), BF16),
                dma((2,)), dma((2,)), dma((2,)), dma((CREDITS,)), dma((2,)), dma((chunks,)), dma((2,)), dma((chunks,)),
                dma((2,)), dma((chunks,)), dma((2,)), dma((chunks,)), dma((2,)), dma((2,)), dma((chunks,)), dma((2,)),
                dma((chunks, 2)), dma, dma((chunks, 2)), dma, dma, pltpu.SemaphoreType.REGULAR,
            ],
            compiler_params=pltpu.CompilerParams(has_side_effects=True, vmem_limit_bytes=66 * 1000 * 1000),
        )(a, g)

    return jax.shard_map(step, mesh=mesh, in_specs=(P(("rep", "dp")), P(("rep", "dp"))), out_specs=P("rep"),
                         check_vma=False)
```

time: 947 us -> 257 us (0.27)
  blocking collectives: 826 us -> 0 us
  Pallas kernels: 0 us -> 236 us
  matrix products: 120 us -> 0 us
  local copies, waits for them, and re-layouts: 0 us -> 21.2 us
    dot_general x1 -> x0, blocking collectives: 826 us -> none  [step(): jnp.einsum('rsntd,rsntf->rndf', a, g, preferred_element_type=jnp.float32)]
    pallas_call x0 -> x1, Pallas kernels: none -> 236 us  [step(): pl.pallas_call(functools.partial(kernel, width, stage), out_shape=jax.Sha...]
    dot_general x1 -> x0, matrix products: 120 us -> none  [step(): jnp.einsum('rsntd,rsntf->rndf', a, g, preferred_element_type=jnp.float32)]
    unnamed x0 -> x1, local copies, waits for them, and re-layouts: none -> 21.2 us
where the time goes in v1:
time: 257 us
  Pallas kernels  236 us (92%)
  local copies, waits for them, and re-layouts  21.2 us (8%)
    pallas_call x1, Pallas kernels, step(): pl.pallas_call(functools.partial(kernel, width, stage), out_shape=jax.Sha...  236 us
    unnamed x1, local copies, waits for them, and re-layouts  21.2 us

profile of v1, /device:TPU:0, one launch (start us, length us, event | category | flops | bytes accessed | tf_op | source)
XLA Modules:
  0.0 257.0 jit_solution(12124891520030547920)
XLA Ops:
  0.0 235.8 %shard_map.28 = bf16[2,1280,5120]{2,1,0:T(8,128)(2,1)} custom-call(bf16[1,2,4096,1280]{3,2,1,0:T(8,128)(2,1)} %a_ref.1, bf16[1,2,4096,5120]{3,2,1,0:T(8,128)(2,1)} %g_ref.1), custom_call_target="tpu_custom_call" | custom-call | tf_op jit(solution)/shard_map/pallas_call | solution.py:345
  235.8 21.2 %copy.4 = bf16[2,1280,5120]{2,1,0:T(8,128)(2,1)} copy(bf16[2,1280,5120]{2,1,0:T(8,128)(2,1)} %shard_map.28) | data formatting | bytes 52428800

commit v2 on v1

v2 whole, which is shorter than its diff:
```python
import functools

import jax
import jax.numpy as jnp
from jax import lax
from jax.experimental import pallas as pl
from jax.experimental.pallas import tpu as pltpu
from jax.sharding import PartitionSpec as P

MESH = pl.DeviceIdType.MESH
F32, BF16 = jnp.float32, jnp.bfloat16
CREDITS = 4
KEPT = 10
LOADS = 6
S1, S2, S3, S4, S5, S6, S7 = 2, 5, 9, 12, 15, 17, 20
HOP = 5


def kernel(width, stage, a_ref, g_ref, o_ref, aT, ast, gbuf, send0, recv0, mL, mK, sendA, recvA, sendR, sendL, sendB,
           recvB, a_sem, g_sem, s0, r0, sA, rA, sR, rR, sL, rL, sB, rB, gBs, gB, gZs, gZ, gAs, gA, gCs, gC, credit):
    me = lax.axis_index("dp")
    core, z = lax.rem(me, 2), lax.rem(me // 2, 4)
    y, x = lax.rem(me // 8, 2), me // 16
    partner = me + 1 - 2 * core
    over_x, over_y = me + 16 * (1 - 2 * x), me + 8 * (1 - 2 * y)
    over_A = over_x * (1 - core) + over_y * core
    over_B = over_y * (1 - core) + over_x * core
    al, be = x * (1 - core) + y * core, y * (1 - core) + x * core
    up, down = me + 2, me - 2
    mats, depth, rows = a_ref.shape[1:]
    per = g_ref.shape[3] // width
    chunks = mats * per
    half, quarter, piece, leaf = rows // 2, rows // 4, rows // 8, rows // 16
    mine, keep = core * half, core * half + al * quarter
    end = 1 - z // 3
    is_end = (z == 0) | (z == 3)

    def at(c, first, count):
        return o_ref.at[index(c, first, count)]

    def index(c, first, count):
        cols = pl.ds(pl.multiple_of(lax.rem(c, per) * width, width), width)
        return c // per, pl.ds(pl.multiple_of(first, leaf), count), cols

    def rdma(src, dst, ssem, rsem, to):
        return pltpu.make_async_remote_copy(src_ref=src, dst_ref=dst, send_sem=ssem, recv_sem=rsem, device_id={"dp": to},
                                            device_id_type=MESH)

    def by_rows(count, block, f):
        @pl.loop(0, count // block)
        def _(i):
            f(pl.multiple_of(i * block, block))

    blk = leaf

    def load_a(n, k):
        return pltpu.make_async_copy(a_ref.at[0, n, pl.ds(pl.multiple_of(k * stage, stage), stage), :],
                                     ast.at[lax.rem(k, LOADS)], a_sem.at[lax.rem(k, LOADS)])

    def load_g(t):
        cols = pl.ds(pl.multiple_of(lax.rem(t, per) * width, width), width)
        return pltpu.make_async_copy(g_ref.at[0, t // per, :, cols], gbuf.at[lax.rem(t, 2)], g_sem.at[lax.rem(t, 2)])

    def start_a(n):
        for k in range(min(LOADS, depth // stage)):
            load_a(n, k).start()

    def transpose_a(n):
        @pl.loop(0, depth // stage)
        def _(k):
            load_a(n, k).wait()
            block = ast[lax.rem(k, LOADS)].T
            for h in (0, 1):
                for j in (0, 1):
                    away = jnp.abs(core - h)
                    to = away * j + (1 - away) * (3 - jnp.abs(al - j))
                    rows_to = pl.ds(pl.multiple_of(to * quarter, quarter), quarter)
                    first = h * half + j * quarter
                    aT[rows_to, pl.ds(pl.multiple_of(k * stage, stage), stage)] = block[first:first + quarter]

            @pl.when(k + LOADS < depth // stage)
            def _():
                load_a(n, k + LOADS).start()

    def product(t, first):
        return jnp.dot(aT[first:first + half, :], gbuf[lax.rem(t, 2)], preferred_element_type=F32)

    def copy0(c):
        return rdma(send0.at[lax.rem(c, 2)], recv0.at[lax.rem(c, CREDITS)], s0.at[lax.rem(c, 2)],
                    r0.at[lax.rem(c, CREDITS)], partner)

    def copyA(c):
        return rdma(sendA.at[lax.rem(c, 2)], recvA.at[c], sA.at[lax.rem(c, 2)], rA.at[c], over_A)

    def copyR(c):
        return rdma(sendR.at[lax.rem(c, 2)], at(c, keep, piece), sR.at[lax.rem(c, 2)], rR.at[c], up)

    def copyL(c):
        return rdma(sendL.at[lax.rem(c, 2)], at(c, keep + piece, piece), sL.at[lax.rem(c, 2)], rL.at[c], down)

    def copyB(c):
        return rdma(sendB.at[lax.rem(c, 2)], recvB.at[c], sB.at[lax.rem(c, 2)], rB.at[c], over_B)

    def reuse(c, copy):
        @pl.when(c >= 2)
        def _():
            copy(c - 2).wait_send()

    def give_leaf(c):
        own = at(c, keep + end * piece + be * leaf, leaf)
        return rdma(own, own, gBs, gB.at[c], over_B)

    def take_leaf(c):
        there = at(c, keep + end * piece + (1 - be) * leaf, leaf)
        return rdma(there, there, gBs, gB.at[c], over_B)

    def stage1(c):
        copy0(c).wait_recv()
        reuse(c, copyA)

        def leaving(i):
            old = recv0[lax.rem(c, CREDITS), pl.ds(pl.multiple_of((1 - al) * quarter + i, blk), blk), :].astype(F32)
            sendA[lax.rem(c, 2), pl.ds(i, blk), :] = (mL[pl.ds(i, blk), :] + old).astype(BF16)

        by_rows(quarter, blk, leaving)
        copyA(c).start()

        def kept(i):
            old = recv0[lax.rem(c, CREDITS), pl.ds(pl.multiple_of(al * quarter + i, blk), blk), :].astype(F32)
            mK[lax.rem(c, KEPT), pl.ds(i, blk), :] += old

        by_rows(quarter, blk, kept)

        @pl.when(c + CREDITS < chunks)
        def _():
            pl.semaphore_signal(credit, inc=1, device_id={"dp": partner}, device_id_type=MESH)

    def pass_on(c, first, arrived, send, copy):
        reuse(c, copy)

        def add(i):
            total = mK[lax.rem(c, KEPT), pl.ds(first + i, blk), :]
            if arrived:
                total = total + o_ref[index(c, keep + first + i, blk)].astype(F32)
            send[lax.rem(c, 2), pl.ds(i, blk), :] = total.astype(BF16)

        by_rows(piece, blk, add)
        copy(c).start()

    def stage2(c):
        copyA(c).wait_recv()

        def add(i):
            mK[lax.rem(c, KEPT), pl.ds(i, blk), :] += recvA[c, pl.ds(i, blk), :].astype(F32)

        by_rows(quarter, blk, add)

        @pl.when(z == 0)
        def _():
            pass_on(c, 0, False, sendR, copyR)

        @pl.when(z == 3)
        def _():
            pass_on(c, piece, False, sendL, copyL)

    def hop_up(c):
        copyR(c).wait_recv()
        pass_on(c, 0, True, sendR, copyR)

    def hop_down(c):
        copyL(c).wait_recv()
        pass_on(c, piece, True, sendL, copyL)

    def stage3(c):
        pl.when(z == 1)(lambda: hop_up(c))
        pl.when(z == 2)(lambda: hop_down(c))

    def stage4(c):
        pl.when(z == 2)(lambda: hop_up(c))
        pl.when(z == 1)(lambda: hop_down(c))

    def finish_z(c, first, copy):
        copy(c).wait_recv()
        reuse(c, copyB)
        away = first + (1 - be) * leaf
        total = mK[lax.rem(c, KEPT), pl.ds(pl.multiple_of(away, leaf), leaf), :]
        sendB[lax.rem(c, 2)] = (total + o_ref[index(c, keep + away, leaf)].astype(F32)).astype(BF16)
        copyB(c).start()
        stay = first + be * leaf
        own = pl.ds(pl.multiple_of(stay, leaf), leaf)
        mK[lax.rem(c, KEPT), own, :] += o_ref[index(c, keep + stay, leaf)].astype(F32)

    def stage5(c):
        pl.when(z == 3)(lambda: finish_z(c, 0, copyR))
        pl.when(z == 0)(lambda: finish_z(c, piece, copyL))

    def stage6(c):
        @pl.when(is_end)
        def _():
            copyB(c).wait_recv()
            stay = end * piece + be * leaf
            total = mK[lax.rem(c, KEPT), pl.ds(pl.multiple_of(stay, leaf), leaf), :] + recvB[c].astype(F32)
            o_ref[index(c, keep + stay, leaf)] = total.astype(BF16)
            give_leaf(c).start()

    def to_z(c, d):
        here = at(c, keep + d * piece, piece)
        return rdma(here, here, gZs.at[d], gZ.at[c, d], up if d else down)

    def to_A(c, d):
        here = at(c, keep + d * piece, piece)
        return rdma(here, here, gAs, gA.at[c, d], over_A)

    def from_A(c, d):
        there = at(c, mine + (1 - al) * quarter + d * piece, piece)
        return rdma(there, there, gAs, gA.at[c, d], over_A)

    def to_core(c, first):
        here = at(c, first, piece)
        return rdma(here, here, gCs, gC, partner)

    def far(d):
        return z if d else 3 - z

    def have(c, d, hop):
        if hop < 3:
            to_z(c, d).start()
        to_A(c, d).start()
        to_core(c, keep + d * piece).start()

    def stage7(hop, c):
        for d in (0, 1):
            @pl.when(far(d) == hop)
            def _(d=d):
                if hop == 0:
                    take_leaf(c).wait_recv()
                else:
                    to_z(c, d).wait_recv()
                have(c, d, hop)

    def stage8(hop, c):
        for d in (0, 1):
            @pl.when(far(d) == hop)
            def _(d=d):
                from_A(c, d).wait_recv()
                to_core(c, mine + (1 - al) * quarter + d * piece).start()

    stages = [(S1, stage1), (S2, stage2), (S3, stage3), (S4, stage4), (S5, stage5), (S6, stage6)]
    stages += [(S7 + HOP * hop, functools.partial(stage7, hop)) for hop in range(4)]
    stages += [(S7 + HOP * hop + HOP, functools.partial(stage8, hop)) for hop in range(4)]
    last = max(lag for lag, _ in stages) // 2

    def serve(t, q):
        for lag, f in sorted(stages, key=lambda s: s[0]):
            if lag % 2 == q:
                c = t - lag // 2

                @pl.when((c >= 0) & (c < chunks))
                def _(f=f, c=c):
                    f(c)

    start_a(0)
    load_g(0).start()

    @pl.loop(0, chunks + last)
    def _(t):
        @pl.when(t + 1 < chunks)
        def _():
            load_g(t + 1).start()

        serve(t, 0)

        @pl.when(t < chunks)
        def _():
            @pl.when(lax.rem(t, per) == 0)
            def _():
                transpose_a(t // per)

            @pl.when((lax.rem(t, per) == per - 1) & (t + 1 < chunks))
            def _():
                start_a(t // per + 1)

            load_g(t).wait()
            reuse(t, copy0)
            send0[lax.rem(t, 2)] = product(t, 0).astype(BF16)

            @pl.when(t >= CREDITS)
            def _():
                pl.semaphore_wait(credit, 1)

            copy0(t).start()

        serve(t, 1)

        @pl.when(t < chunks)
        def _():
            both = product(t, half)
            mL[...] = both[:quarter]
            mK[lax.rem(t, KEPT)] = both[quarter:]

    def rest(first, count):
        return o_ref.at[:, pl.ds(pl.multiple_of(first, leaf), count), :]

    for c in range(chunks - 2, chunks):
        copy0(c).wait_send()
        copyA(c).wait_send()
        pl.when(z < 3)(lambda: copyR(c).wait_send())
        pl.when(z > 0)(lambda: copyL(c).wait_send())

        @pl.when(is_end)
        def _(c=c):
            copyB(c).wait_send()

    @pl.when(is_end)
    def _():
        some = rest(keep, leaf)
        rdma(some, some, gBs, gC, over_B).wait_send()

    for d in (0, 1):
        @pl.when(far(d) < 3)
        def _(d=d):
            some = rest(keep + d * piece, piece)
            rdma(some, some, gZs.at[d], gC, partner).wait_send()

    some = rest(keep, quarter)
    rdma(some, some, gAs, gC, over_A).wait_send()
    some = rest(mine, half)
    rdma(some, some, gCs, gC, partner).wait_send()
    some = rest((1 - core) * half, half)
    rdma(some, some, gCs, gC, partner).wait_recv()


def solution(mesh, width=256, stage=256):
    def step(a, g):
        mats, depth, rows = a.shape[1:]
        columns = g.shape[3]
        chunks = mats * (columns // width)
        half, quarter, piece, leaf = rows // 2, rows // 4, rows // 8, rows // 16
        dma = pltpu.SemaphoreType.DMA
        return pl.pallas_call(
            functools.partial(kernel, width, stage),
            out_shape=pltpu.VMEM((mats, rows, columns), BF16),
            in_specs=[pl.BlockSpec(memory_space=pl.ANY)] * 2,
            out_specs=pl.BlockSpec(memory_space=pltpu.VMEM),
            scratch_shapes=[
                pltpu.VMEM((rows, depth), BF16),
                pltpu.VMEM((LOADS, stage, rows), BF16),
                pltpu.VMEM((2, depth, width), BF16),
                pltpu.VMEM((2, half, width), BF16),
                pltpu.VMEM((CREDITS, half, width), BF16),
                pltpu.VMEM((quarter, width), F32),
                pltpu.VMEM((KEPT, quarter, width), F32),
                pltpu.VMEM((2, quarter, width), BF16),
                pltpu.VMEM((chunks, quarter, width), BF16),
                pltpu.VMEM((2, piece, width), BF16),
                pltpu.VMEM((2, piece, width), BF16),
                pltpu.VMEM((2, leaf, width), BF16),
                pltpu.VMEM((chunks, leaf, width), BF16),
                dma((LOADS,)), dma((2,)), dma((2,)), dma((CREDITS,)), dma((2,)), dma((chunks,)), dma((2,)),
                dma((chunks,)), dma((2,)), dma((chunks,)), dma((2,)), dma((chunks,)), dma, dma((chunks,)), dma((2,)),
                dma((chunks, 2)), dma, dma((chunks, 2)), dma, dma, pltpu.SemaphoreType.REGULAR,
            ],
            compiler_params=pltpu.CompilerParams(has_side_effects=True, vmem_limit_bytes=40 * 1000 * 1000),
        )(a, g)

    return jax.shard_map(step, mesh=mesh, in_specs=(P(("rep", "dp")), P(("rep", "dp"))), out_specs=P("rep"),
                         check_vma=False)
```

time: 257 us -> 229 us (0.89)
  Pallas kernels: 236 us -> 220 us
  local copies, waits for them, and re-layouts: 21.2 us -> 9.27 us
    pallas_call x1, Pallas kernels: 236 us -> 220 us  [step(): pl.pallas_call(functools.partial(kernel, width, stage), out_shape=pltpu.V...]
    unnamed x1, local copies, waits for them, and re-layouts: 21.2 us -> 9.27 us
where the time goes in v2:
time: 229 us
  Pallas kernels  220 us (96%)
  local copies, waits for them, and re-layouts  9.27 us (4%)
    pallas_call x1, Pallas kernels, step(): pl.pallas_call(functools.partial(kernel, width, stage), out_shape=pltpu.V...  220 us
    unnamed x1, local copies, waits for them, and re-layouts  9.27 us

profile of v2, /device:TPU:0, one launch (start us, length us, event | category | flops | bytes accessed | tf_op | source)
XLA Modules:
  0.0 229.1 jit_solution(6118110940308944233)
XLA Ops:
  0.0 219.8 %shard_map.28 = bf16[2,1280,5120]{2,1,0:T(8,128)(2,1)S(1)} custom-call(bf16[1,2,4096,1280]{3,2,1,0:T(8,128)(2,1)} %a_ref.1, bf16[1,2,4096,5120]{3,2,1,0:T(8,128)(2,1)} %g_ref.1), custom_call_target="tpu_custom_call" | custom-call | tf_op jit(solution)/shard_map/pallas_call | solution.py:340
  219.8 9.3 %copy.4 = bf16[2,1280,5120]{2,1,0:T(8,128)(2,1)} copy(bf16[2,1280,5120]{2,1,0:T(8,128)(2,1)S(1)} %shard_map.28) | data formatting | bytes 52428800

commit v3 on v2

--- a/solution.py
+++ b/solution.py
@@ -9,8 +9,8 @@
 
 MESH = pl.DeviceIdType.MESH
 F32, BF16 = jnp.float32, jnp.bfloat16
-CREDITS = 4
-KEPT = 10
+CREDITS = 8
+KEPT = 16
 LOADS = 6
 S1, S2, S3, S4, S5, S6, S7 = 2, 5, 9, 12, 15, 17, 20
 HOP = 5
@@ -38,28 +38,25 @@
     def at(c, first, count):
         return o_ref.at[index(c, first, count)]
 
+    def place(c):
+        n = c // per if isinstance(c, int) else sum((c >= m * per).astype(jnp.int32) for m in range(1, mats))
+        return n, pl.ds(pl.multiple_of((c - n * per) * width, width), width)
+
     def index(c, first, count):
-        cols = pl.ds(pl.multiple_of(lax.rem(c, per) * width, width), width)
-        return c // per, pl.ds(pl.multiple_of(first, leaf), count), cols
+        n, cols = place(c)
+        return n, pl.ds(pl.multiple_of(first, leaf), count), cols
 
     def rdma(src, dst, ssem, rsem, to):
         return pltpu.make_async_remote_copy(src_ref=src, dst_ref=dst, send_sem=ssem, recv_sem=rsem, device_id={"dp": to},
                                             device_id_type=MESH)
 
-    def by_rows(count, block, f):
-        @pl.loop(0, count // block)
-        def _(i):
-            f(pl.multiple_of(i * block, block))
-
-    blk = leaf
-
     def load_a(n, k):
         return pltpu.make_async_copy(a_ref.at[0, n, pl.ds(pl.multiple_of(k * stage, stage), stage), :],
                                      ast.at[lax.rem(k, LOADS)], a_sem.at[lax.rem(k, LOADS)])
 
     def load_g(t):
-        cols = pl.ds(pl.multiple_of(lax.rem(t, per) * width, width), width)
-        return pltpu.make_async_copy(g_ref.at[0, t // per, :, cols], gbuf.at[lax.rem(t, 2)], g_sem.at[lax.rem(t, 2)])
+        n, cols = place(t)
+        return pltpu.make_async_copy(g_ref.at[0, n, :, cols], gbuf.at[lax.rem(t, 2)], g_sem.at[lax.rem(t, 2)])
 
     def start_a(n):
         for k in range(min(LOADS, depth // stage)):
@@ -117,59 +114,48 @@
     def stage1(c):
         copy0(c).wait_recv()
         reuse(c, copyA)
-
-        def leaving(i):
-            old = recv0[lax.rem(c, CREDITS), pl.ds(pl.multiple_of((1 - al) * quarter + i, blk), blk), :].astype(F32)
-            sendA[lax.rem(c, 2), pl.ds(i, blk), :] = (mL[pl.ds(i, blk), :] + old).astype(BF16)
-
-        by_rows(quarter, blk, leaving)
+        for i in (0, piece):
+            old = recv0[lax.rem(c, CREDITS), pl.ds(pl.multiple_of((1 - al) * quarter + i, piece), piece), :]
+            sendA[lax.rem(c, 2), i:i + piece, :] = (mL[i:i + piece, :] + old.astype(F32)).astype(BF16)
         copyA(c).start()
 
-        def kept(i):
-            old = recv0[lax.rem(c, CREDITS), pl.ds(pl.multiple_of(al * quarter + i, blk), blk), :].astype(F32)
-            mK[lax.rem(c, KEPT), pl.ds(i, blk), :] += old
-
-        by_rows(quarter, blk, kept)
-
-        @pl.when(c + CREDITS < chunks)
-        def _():
-            pl.semaphore_signal(credit, inc=1, device_id={"dp": partner}, device_id_type=MESH)
-
-    def pass_on(c, first, arrived, send, copy):
+    def total(c, i):
+        old = recv0[lax.rem(c, CREDITS), pl.ds(pl.multiple_of(al * quarter + i, piece), piece), :]
+        here = mK[lax.rem(c, KEPT), i:i + piece, :] + old.astype(F32)
+        return here + recvA[c, i:i + piece, :].astype(F32)
+
+    def first_hop(c, i, send, copy):
         reuse(c, copy)
-
-        def add(i):
-            total = mK[lax.rem(c, KEPT), pl.ds(first + i, blk), :]
-            if arrived:
-                total = total + o_ref[index(c, keep + first + i, blk)].astype(F32)
-            send[lax.rem(c, 2), pl.ds(i, blk), :] = total.astype(BF16)
-
-        by_rows(piece, blk, add)
+        send[lax.rem(c, 2)] = total(c, i).astype(BF16)
         copy(c).start()
+        mK[lax.rem(c, KEPT), piece - i:2 * piece - i, :] = total(c, piece - i)
 
     def stage2(c):
         copyA(c).wait_recv()
-
-        def add(i):
-            mK[lax.rem(c, KEPT), pl.ds(i, blk), :] += recvA[c, pl.ds(i, blk), :].astype(F32)
-
-        by_rows(quarter, blk, add)
-
-        @pl.when(z == 0)
-        def _():
-            pass_on(c, 0, False, sendR, copyR)
-
-        @pl.when(z == 3)
-        def _():
-            pass_on(c, piece, False, sendL, copyL)
+        pl.when(z == 0)(lambda: first_hop(c, 0, sendR, copyR))
+        pl.when(z == 3)(lambda: first_hop(c, piece, sendL, copyL))
+
+        @pl.when((z == 1) | (z == 2))
+        def _():
+            for i in (0, piece):
+                mK[lax.rem(c, KEPT), i:i + piece, :] = total(c, i)
+
+        @pl.when(c + CREDITS < chunks)
+        def _():
+            pl.semaphore_signal(credit, inc=1, device_id={"dp": partner}, device_id_type=MESH)
+
+    def pass_on(c, first, send, copy):
+        copy(c).wait_recv()
+        reuse(c, copy)
+        here = mK[lax.rem(c, KEPT), first:first + piece, :]
+        send[lax.rem(c, 2)] = (here + o_ref[index(c, keep + first, piece)].astype(F32)).astype(BF16)
+        copy(c).start()
 
     def hop_up(c):
-        copyR(c).wait_recv()
-        pass_on(c, 0, True, sendR, copyR)
+        pass_on(c, 0, sendR, copyR)
 
     def hop_down(c):
-        copyL(c).wait_recv()
-        pass_on(c, piece, True, sendL, copyL)
+        pass_on(c, piece, sendL, copyL)
 
     def stage3(c):
         pl.when(z == 1)(lambda: hop_up(c))
@@ -215,8 +201,8 @@
         there = at(c, mine + (1 - al) * quarter + d * piece, piece)
         return rdma(there, there, gAs, gA.at[c, d], over_A)
 
-    def to_core(c, first):
-        here = at(c, first, piece)
+    def to_core(c):
+        here = at(c, mine, half)
         return rdma(here, here, gCs, gC, partner)
 
     def far(d):
@@ -226,7 +212,6 @@
         if hop < 3:
             to_z(c, d).start()
         to_A(c, d).start()
-        to_core(c, keep + d * piece).start()
 
     def stage7(hop, c):
         for d in (0, 1):
@@ -243,7 +228,11 @@
             @pl.when(far(d) == hop)
             def _(d=d):
                 from_A(c, d).wait_recv()
-                to_core(c, mine + (1 - al) * quarter + d * piece).start()
+
+        if hop >= 2:
+            @pl.when((jnp.maximum(far(0), far(1)) == hop))
+            def _():
+                to_core(c).start()
 
     stages = [(S1, stage1), (S2, stage2), (S3, stage3), (S4, stage4), (S5, stage5), (S6, stage6)]
     stages += [(S7 + HOP * hop, functools.partial(stage7, hop)) for hop in range(4)]
@@ -261,6 +250,20 @@
 
     start_a(0)
     load_g(0).start()
+    barrier = pltpu.get_barrier_semaphore()
+    for other in (partner, over_A, over_B):
+        pl.semaphore_signal(barrier, inc=1, device_id={"dp": other}, device_id_type=MESH)
+
+    @pl.when(z < 3)
+    def _():
+        pl.semaphore_signal(barrier, inc=1, device_id={"dp": up}, device_id_type=MESH)
+
+    @pl.when(z > 0)
+    def _():
+        pl.semaphore_signal(barrier, inc=1, device_id={"dp": down}, device_id_type=MESH)
+
+    transpose_a(0)
+    pl.semaphore_wait(barrier, 3 + (z < 3).astype(jnp.int32) + (z > 0).astype(jnp.int32))
 
     @pl.loop(0, chunks + last)
     def _(t):
@@ -272,13 +275,9 @@
 
         @pl.when(t < chunks)
         def _():
-            @pl.when(lax.rem(t, per) == 0)
-            def _():
-                transpose_a(t // per)
-
-            @pl.when((lax.rem(t, per) == per - 1) & (t + 1 < chunks))
-            def _():
-                start_a(t // per + 1)
+            for n in range(1, mats):
+                pl.when(t == n * per)(functools.partial(transpose_a, n))
+                pl.when(t == n * per - 1)(functools.partial(start_a, n))
 
             load_g(t).wait()
             reuse(t, copy0)
@@ -360,7 +359,7 @@
                 dma((chunks,)), dma((2,)), dma((chunks,)), dma((2,)), dma((chunks,)), dma, dma((chunks,)), dma((2,)),
                 dma((chunks, 2)), dma, dma((chunks, 2)), dma, dma, pltpu.SemaphoreType.REGULAR,
             ],
-            compiler_params=pltpu.CompilerParams(has_side_effects=True, vmem_limit_bytes=40 * 1000 * 1000),
+            compiler_params=pltpu.CompilerParams(collective_id=0, has_side_effects=True, vmem_limit_bytes=40 * 1000 * 1000),
         )(a, g)
 
     return jax.shard_map(step, mesh=mesh, in_specs=(P(("rep", "dp")), P(("rep", "dp"))), out_specs=P("rep"),

time: 229 us -> 221 us (0.965)
  Pallas kernels: 220 us -> 211 us
    pallas_call x1, Pallas kernels: 220 us -> 211 us  [step(): pl.pallas_call(functools.partial(kernel, width, stage), out_shape=pltpu.V...]
where the time goes in v3:
time: 221 us
  Pallas kernels  211 us (95%)
  local copies, waits for them, and re-layouts  9.27 us (4%)
    pallas_call x1, Pallas kernels, step(): pl.pallas_call(functools.partial(kernel, width, stage), out_shape=pltpu.V...  211 us
    unnamed x1, local copies, waits for them, and re-layouts  9.27 us

profile of v3, /device:TPU:0, one launch (start us, length us, event | category | flops | bytes accessed | tf_op | source)
XLA Modules:
  0.0 220.7 jit_solution(16525167546848685905)
XLA Ops:
  0.0 211.4 %shard_map.28 = bf16[2,1280,5120]{2,1,0:T(8,128)(2,1)S(1)} custom-call(bf16[1,2,4096,1280]{3,2,1,0:T(8,128)(2,1)} %a_ref.1, bf16[1,2,4096,5120]{3,2,1,0:T(8,128)(2,1)} %g_ref.1), custom_call_target="tpu_custom_call" | custom-call | tf_op jit(solution)/shard_map/pallas_call | solution.py:339
  211.4 9.3 %copy.4 = bf16[2,1280,5120]{2,1,0:T(8,128)(2,1)} copy(bf16[2,1280,5120]{2,1,0:T(8,128)(2,1)S(1)} %shard_map.28) | data formatting | bytes 52428800

commit v4 on v3

--- a/solution.py
+++ b/solution.py
@@ -11,13 +11,18 @@
 F32, BF16 = jnp.float32, jnp.bfloat16
 CREDITS = 8
 KEPT = 16
-LOADS = 6
-S1, S2, S3, S4, S5, S6, S7 = 2, 5, 9, 12, 15, 17, 20
-HOP = 5
+LOADS = 8
+S1, S2, S3, S4, S5, S6 = 2, 5, 9, 12, 15, 17
+S7 = 20, 25, 30, 36
+S8 = 27, 32, 35, 46
+
+
+def wide(c):
+    return (lax.rem(c, 4) == 2) & (c < 22)
 
 
 def kernel(width, stage, a_ref, g_ref, o_ref, aT, ast, gbuf, send0, recv0, mL, mK, sendA, recvA, sendR, sendL, sendB,
-           recvB, a_sem, g_sem, s0, r0, sA, rA, sR, rR, sL, rL, sB, rB, gBs, gB, gZs, gZ, gAs, gA, gCs, gC, credit):
+           recvB, a_sem, g_sem, s0, r0, sA, rA, sR, rR, sL, rL, sB, rB, gBs, gB, gZs, gZ, gNs, gAs, gA, gCs, gC, credit):
     me = lax.axis_index("dp")
     core, z = lax.rem(me, 2), lax.rem(me // 2, 4)
     y, x = lax.rem(me // 8, 2), me // 16
@@ -50,34 +55,40 @@
         return pltpu.make_async_remote_copy(src_ref=src, dst_ref=dst, send_sem=ssem, recv_sem=rsem, device_id={"dp": to},
                                             device_id_type=MESH)
 
-    def load_a(n, k):
-        return pltpu.make_async_copy(a_ref.at[0, n, pl.ds(pl.multiple_of(k * stage, stage), stage), :],
-                                     ast.at[lax.rem(k, LOADS)], a_sem.at[lax.rem(k, LOADS)])
+    blocks = depth // stage
+
+    def load_a(n, i):
+        late = int(i >= blocks) if isinstance(i, int) else (i >= blocks).astype(jnp.int32)
+        k = i - late * blocks
+        cols = pl.ds(pl.multiple_of((core * late + (1 - core) * (1 - late)) * half, half), half)
+        slot = lax.rem(i, LOADS)
+        return pltpu.make_async_copy(a_ref.at[0, n, pl.ds(pl.multiple_of(k * stage, stage), stage), cols], ast.at[slot],
+                                     a_sem.at[slot])
 
     def load_g(t):
         n, cols = place(t)
         return pltpu.make_async_copy(g_ref.at[0, n, :, cols], gbuf.at[lax.rem(t, 2)], g_sem.at[lax.rem(t, 2)])
 
     def start_a(n):
-        for k in range(min(LOADS, depth // stage)):
-            load_a(n, k).start()
-
-    def transpose_a(n):
-        @pl.loop(0, depth // stage)
-        def _(k):
-            load_a(n, k).wait()
-            block = ast[lax.rem(k, LOADS)].T
-            for h in (0, 1):
+        for i in range(min(LOADS, 2 * blocks)):
+            load_a(n, i).start()
+
+    def transpose_a(n, late):
+        @pl.loop(late * blocks, (late + 1) * blocks)
+        def _(i):
+            load_a(n, i).wait()
+            block = ast[lax.rem(i, LOADS)].T
+            cols = pl.ds(pl.multiple_of((i - late * blocks) * stage, stage), stage)
+            if late:
                 for j in (0, 1):
-                    away = jnp.abs(core - h)
-                    to = away * j + (1 - away) * (3 - jnp.abs(al - j))
-                    rows_to = pl.ds(pl.multiple_of(to * quarter, quarter), quarter)
-                    first = h * half + j * quarter
-                    aT[rows_to, pl.ds(pl.multiple_of(k * stage, stage), stage)] = block[first:first + quarter]
-
-            @pl.when(k + LOADS < depth // stage)
+                    to = pl.ds(pl.multiple_of((3 - jnp.abs(al - j)) * quarter, quarter), quarter)
+                    aT[to, cols] = block[j * quarter:(j + 1) * quarter]
+            else:
+                aT[:half, cols] = block
+
+            @pl.when(i + LOADS < 2 * blocks)
             def _():
-                load_a(n, k + LOADS).start()
+                load_a(n, i + LOADS).start()
 
     def product(t, first):
         return jnp.dot(aT[first:first + half, :], gbuf[lax.rem(t, 2)], preferred_element_type=F32)
@@ -195,11 +206,11 @@
 
     def to_A(c, d):
         here = at(c, keep + d * piece, piece)
-        return rdma(here, here, gAs, gA.at[c, d], over_A)
+        return rdma(here, here, gAs.at[d], gA.at[c, d], over_A)
 
     def from_A(c, d):
         there = at(c, mine + (1 - al) * quarter + d * piece, piece)
-        return rdma(there, there, gAs, gA.at[c, d], over_A)
+        return rdma(there, there, gNs.at[d], gA.at[c, d], up if d else down)
 
     def to_core(c):
         here = at(c, mine, half)
@@ -211,7 +222,10 @@
     def have(c, d, hop):
         if hop < 3:
             to_z(c, d).start()
-        to_A(c, d).start()
+        if hop == 0:
+            to_A(c, d).start()
+        else:
+            pl.when(jnp.logical_not(wide(c)))(lambda: to_A(c, d).start())
 
     def stage7(hop, c):
         for d in (0, 1):
@@ -228,6 +242,8 @@
             @pl.when(far(d) == hop)
             def _(d=d):
                 from_A(c, d).wait_recv()
+                if hop < 3:
+                    pl.when(wide(c))(lambda: from_A(c, d).start())
 
         if hop >= 2:
             @pl.when((jnp.maximum(far(0), far(1)) == hop))
@@ -235,8 +251,8 @@
                 to_core(c).start()
 
     stages = [(S1, stage1), (S2, stage2), (S3, stage3), (S4, stage4), (S5, stage5), (S6, stage6)]
-    stages += [(S7 + HOP * hop, functools.partial(stage7, hop)) for hop in range(4)]
-    stages += [(S7 + HOP * hop + HOP, functools.partial(stage8, hop)) for hop in range(4)]
+    stages += [(lag, functools.partial(stage7, hop)) for hop, lag in enumerate(S7)]
+    stages += [(lag, functools.partial(stage8, hop)) for hop, lag in enumerate(S8)]
     last = max(lag for lag, _ in stages) // 2
 
     def serve(t, q):
@@ -262,7 +278,7 @@
     def _():
         pl.semaphore_signal(barrier, inc=1, device_id={"dp": down}, device_id_type=MESH)
 
-    transpose_a(0)
+    transpose_a(0, 0)
     pl.semaphore_wait(barrier, 3 + (z < 3).astype(jnp.int32) + (z > 0).astype(jnp.int32))
 
     @pl.loop(0, chunks + last)
@@ -276,7 +292,7 @@
         @pl.when(t < chunks)
         def _():
             for n in range(1, mats):
-                pl.when(t == n * per)(functools.partial(transpose_a, n))
+                pl.when(t == n * per)(functools.partial(transpose_a, n, 0))
                 pl.when(t == n * per - 1)(functools.partial(start_a, n))
 
             load_g(t).wait()
@@ -293,6 +309,9 @@
 
         @pl.when(t < chunks)
         def _():
+            for n in range(mats):
+                pl.when(t == n * per)(functools.partial(transpose_a, n, 1))
+
             both = product(t, half)
             mL[...] = both[:quarter]
             mK[lax.rem(t, KEPT)] = both[quarter:]
@@ -315,14 +334,29 @@
         some = rest(keep, leaf)
         rdma(some, some, gBs, gC, over_B).wait_send()
 
+    wides = sum(c % 4 == 2 and c < 22 for c in range(chunks))
+
+    def several(d, count):
+        return o_ref.at[:, pl.ds(pl.multiple_of(keep + d * piece, piece), piece), pl.ds(0, count * width // mats)]
+
     for d in (0, 1):
         @pl.when(far(d) < 3)
         def _(d=d):
-            some = rest(keep + d * piece, piece)
+            some = several(d, chunks)
             rdma(some, some, gZs.at[d], gC, partner).wait_send()
-
-    some = rest(keep, quarter)
-    rdma(some, some, gAs, gC, over_A).wait_send()
+            some = several(d, wides)
+            rdma(some, some, gNs.at[d], gC, partner).wait_send()
+
+        @pl.when(far(d) == 0)
+        def _(d=d):
+            some = several(d, chunks)
+            rdma(some, some, gAs.at[d], gC, over_A).wait_send()
+
+        @pl.when(far(d) > 0)
+        def _(d=d):
+            some = several(d, chunks - wides)
+            rdma(some, some, gAs.at[d], gC, over_A).wait_send()
+
     some = rest(mine, half)
     rdma(some, some, gCs, gC, partner).wait_send()
     some = rest((1 - core) * half, half)
@@ -343,7 +377,7 @@
             out_specs=pl.BlockSpec(memory_space=pltpu.VMEM),
             scratch_shapes=[
                 pltpu.VMEM((rows, depth), BF16),
-                pltpu.VMEM((LOADS, stage, rows), BF16),
+                pltpu.VMEM((LOADS, stage, half), BF16),
                 pltpu.VMEM((2, depth, width), BF16),
                 pltpu.VMEM((2, half, width), BF16),
                 pltpu.VMEM((CREDITS, half, width), BF16),
@@ -357,7 +391,8 @@
                 pltpu.VMEM((chunks, leaf, width), BF16),
                 dma((LOADS,)), dma((2,)), dma((2,)), dma((CREDITS,)), dma((2,)), dma((chunks,)), dma((2,)),
                 dma((chunks,)), dma((2,)), dma((chunks,)), dma((2,)), dma((chunks,)), dma, dma((chunks,)), dma((2,)),
-                dma((chunks, 2)), dma, dma((chunks, 2)), dma, dma, pltpu.SemaphoreType.REGULAR,
+                dma((chunks, 2)), dma((2,)), dma((2,)), dma((chunks, 2)), dma, dma,
+                pltpu.SemaphoreType.REGULAR,
             ],
             compiler_params=pltpu.CompilerParams(collective_id=0, has_side_effects=True, vmem_limit_bytes=40 * 1000 * 1000),
         )(a, g)

time: 221 us -> 218 us (0.986)
    pallas_call x1, Pallas kernels: 211 us -> 209 us  [step(): pl.pallas_call(functools.partial(kernel, width, stage), out_shape=pltpu.V...]
where the time goes in v4:
time: 218 us
  Pallas kernels  209 us (96%)
  local copies, waits for them, and re-layouts  9.27 us (4%)
    pallas_call x1, Pallas kernels, step(): pl.pallas_call(functools.partial(kernel, width, stage), out_shape=pltpu.V...  209 us
    unnamed x1, local copies, waits for them, and re-layouts  9.27 us

profile of v4, /device:TPU:0, one launch (start us, length us, event | category | flops | bytes accessed | tf_op | source)
XLA Modules:
  0.0 218.3 jit_solution(1560250612913982859)
XLA Ops:
  0.0 209.0 %shard_map.28 = bf16[2,1280,5120]{2,1,0:T(8,128)(2,1)S(1)} custom-call(bf16[1,2,4096,1280]{3,2,1,0:T(8,128)(2,1)} %a_ref.1, bf16[1,2,4096,5120]{3,2,1,0:T(8,128)(2,1)} %g_ref.1), custom_call_target="tpu_custom_call" | custom-call | tf_op jit(solution)/shard_map/pallas_call | solution.py:373
  209.0 9.3 %copy.4 = bf16[2,1280,5120]{2,1,0:T(8,128)(2,1)} copy(bf16[2,1280,5120]{2,1,0:T(8,128)(2,1)S(1)} %shard_map.28) | data formatting | bytes 52428800

commit v5 on v4

--- a/solution.py
+++ b/solution.py
@@ -11,10 +11,10 @@
 F32, BF16 = jnp.float32, jnp.bfloat16
 CREDITS = 8
 KEPT = 16
-LOADS = 8
-S1, S2, S3, S4, S5, S6 = 2, 5, 9, 12, 15, 17
-S7 = 20, 25, 30, 36
-S8 = 27, 32, 35, 46
+LOADS = 16
+S1, S2, S3, S4, S5, S6 = 2, 5, 8, 11, 14, 17
+S7 = 19, 24, 29, 40
+S8 = 30, 33, 36, 49
 
 
 def wide(c):

time: 218 us -> 217 us (level)
  no operation moved by 1% of the time
where the time goes in v5:
time: 217 us
  Pallas kernels  208 us (96%)
  local copies, waits for them, and re-layouts  9.27 us (4%)
    pallas_call x1, Pallas kernels, step(): pl.pallas_call(functools.partial(kernel, width, stage), out_shape=pltpu.V...  208 us
    unnamed x1, local copies, waits for them, and re-layouts  9.27 us

profile of v5, /device:TPU:0, one launch (start us, length us, event | category | flops | bytes accessed | tf_op | source)
XLA Modules:
  0.0 217.1 jit_solution(13597538546021932281)
XLA Ops:
  0.0 207.9 %shard_map.28 = bf16[2,1280,5120]{2,1,0:T(8,128)(2,1)S(1)} custom-call(bf16[1,2,4096,1280]{3,2,1,0:T(8,128)(2,1)} %a_ref.1, bf16[1,2,4096,5120]{3,2,1,0:T(8,128)(2,1)} %g_ref.1), custom_call_target="tpu_custom_call" | custom-call | tf_op jit(solution)/shard_map/pallas_call | solution.py:373
  207.9 9.3 %copy.4 = bf16[2,1280,5120]{2,1,0:T(8,128)(2,1)} copy(bf16[2,1280,5120]{2,1,0:T(8,128)(2,1)S(1)} %shard_map.28) | data formatting | bytes 52428800

commit v6 on v5

--- a/solution.py
+++ b/solution.py
@@ -13,8 +13,9 @@
 KEPT = 16
 LOADS = 16
 S1, S2, S3, S4, S5, S6 = 2, 5, 8, 11, 14, 17
-S7 = 19, 24, 29, 40
-S8 = 30, 33, 36, 49
+S7 = 20, 25, 30, 41
+S8 = 30, 35, 38, 52
+ORDER = 3, 7, 9, 11, 0, 1, 8, 13, 4, 10, 6, 12, 5, 2
 
 
 def wide(c):
@@ -256,7 +257,7 @@
     last = max(lag for lag, _ in stages) // 2
 
     def serve(t, q):
-        for lag, f in sorted(stages, key=lambda s: s[0]):
+        for lag, f in (stages[i] for i in ORDER):
             if lag % 2 == q:
                 c = t - lag // 2
 

time: 217 us -> 217 us (level)
  no operation moved by 1% of the time
where the time goes in v6:
time: 217 us; the launch traced here: 216 us
  Pallas kernels  207 us (95%)
  local copies, waits for them, and re-layouts  9.27 us (4%)
    pallas_call x1, Pallas kernels, step(): pl.pallas_call(functools.partial(kernel, width, stage), out_shape=pltpu.V...  207 us
    unnamed x1, local copies, waits for them, and re-layouts  9.27 us

profile of v6, /device:TPU:0, one launch (start us, length us, event | category | flops | bytes accessed | tf_op | source)
XLA Modules:
  0.0 216.4 jit_solution(931350661272523772)
XLA Ops:
  0.0 207.2 %shard_map.28 = bf16[2,1280,5120]{2,1,0:T(8,128)(2,1)S(1)} custom-call(bf16[1,2,4096,1280]{3,2,1,0:T(8,128)(2,1)} %a_ref.1, bf16[1,2,4096,5120]{3,2,1,0:T(8,128)(2,1)} %g_ref.1), custom_call_target="tpu_custom_call" | custom-call | tf_op jit(solution)/shard_map/pallas_call | solution.py:374
  207.2 9.3 %copy.4 = bf16[2,1280,5120]{2,1,0:T(8,128)(2,1)} copy(bf16[2,1280,5120]{2,1,0:T(8,128)(2,1)S(1)} %shard_map.28) | data formatting | bytes 52428800
